TPU v7x, 8 devices: a whole 2x2x1 slice. The times are simulated.
8 devices in a mesh: data: 1 (over z), row: 2 (over y), col: 4 (over x, core).
Axes of the slice: x: 2, y: 2, z: 1, core: 2. Of those that a mesh axis runs over, the one named last changes fastest.
Arguments:
- tokens: bfloat16 [1536, 2048], P(('data', 'row', 'col'))
- expert_ids: int32 [1536, 8], P(('data', 'row', 'col'))
- gate_weights: float32 [1536, 8], P(('data', 'row', 'col'))
- w_in: bfloat16 [64, 2048, 1024], P(('row', 'col'))
- w_out: bfloat16 [64, 1024, 2048], P(('row', 'col'))
Outputs:
- output: bfloat16 [1536, 2048], P(('data', 'row', 'col'))
All inputs are finite; a program needn't handle non-finite values.
Results may differ from a plain program's by a relative error of at most 0.00449034.
Values are sent between devices in bfloat16 or wider.
A program may use at most 1 GiB of HBM per device.

v0:
```python
import functools
import math

import jax
import jax.numpy as jnp
from jax import lax
from jax.experimental import pallas as pl
from jax.experimental.pallas import tpu as pltpu
from jax.sharding import PartitionSpec as P

GRID_AXES = ('row', 'col')
MESH = pl.DeviceIdType.MESH
BF = jnp.bfloat16
F32 = jnp.float32
WIN = 64
LEAD = 2
AG_KINDS = ((0, None, 1), (0, None, 2), (0, None, 4), (2, 0, 4), (4, 1, 2), (2, None, 1), (4, None, 1), (6, 0, 1), (6, 1, 1))
RETURN_ORDER = (6, 2, 4, 0)


def gelu_tanh(x):
    scale = (2.0 / math.pi) ** 0.5
    h = 0.5 * x
    return h + h * jnp.tanh(x * (scale + (scale * 0.044715) * (x * x)))


def moe_kernel(cfg, ids_hbm, gate_hbm, tok_hbm, wi_hbm, wo_hbm, out_hbm,
               ids_all, gate_all, tok_all, pmat, cmat, hacc, hbf, wi, wo, obuf, d2d_out, d2d_in, out1, in1, out2, in2, kept, own, outv,
               ids_v, gate_v, slot_buf, zbuf, start_v, start_s,
               tok_sem, wi_sem, wo_sem, ms_sem, mr_sem, gs_sem, gr_sem, as_sem, ar_sem, ds_sem, dr_sem,
               s1_sem, r1_sem, s2_sem, rf_sem, st_sem, out_sem, id_sem, gate_sem):
    tok_dev, cap, nexp, nch, wd, ff = cfg
    ntok = 8 * tok_dev
    half = tok_dev // 2
    i = lax.axis_index('row')
    j = lax.axis_index('col')
    j_flip = j + 1 - 2 * lax.rem(j, 2)

    def rel(r):
        jj = j_flip if r & 1 else j
        if r & 2:
            jj = lax.rem(jj + 2, 4)
        ii = lax.rem(i + 1, 2) if r & 4 else i
        return ii, jj

    def dev(r):
        ii, jj = rel(r)
        return {'row': ii, 'col': jj}

    def gidx(r):
        ii, jj = rel(r)
        return ii * 4 + jj

    def rows_of(r):
        return pl.ds(pl.multiple_of(gidx(r) * tok_dev, 64), tok_dev)

    me = gidx(0)

    def tok_copy(c):
        return pltpu.make_async_copy(tok_hbm.at[:, pl.ds(c * wd, wd)], tok_all.at[c, rows_of(0), :], tok_sem.at[c])

    nh = nexp // 2

    def wi_copy(c, p):
        return pltpu.make_async_copy(wi_hbm.at[p * nh:(p + 1) * nh, pl.ds(c * wd, wd), :], wi.at[p], wi_sem.at[p])

    def wo_copy(c, p):
        return pltpu.make_async_copy(wo_hbm.at[p * nh:(p + 1) * nh, :, pl.ds(pl.multiple_of(c * wd, wd), wd)], wo.at[p],
                                     wo_sem.at[p])

    def out_copy(c):
        return pltpu.make_async_copy(outv.at[c], out_hbm.at[:, pl.ds(pl.multiple_of(c * wd, wd), wd)], out_sem.at[c])

    bar = pltpu.get_barrier_semaphore()
    for r in range(1, 8):
        pl.semaphore_signal(bar, inc=1, device_id=dev(r), device_id_type=MESH)
    ids_in = pltpu.make_async_copy(ids_hbm, ids_v, id_sem)
    gate_in = pltpu.make_async_copy(gate_hbm, gate_v, gate_sem)
    ids_in.start()
    gate_in.start()
    for c in range(nch):
        tok_copy(c).start()
    ids_all[me] = jnp.zeros((8, 256), jnp.int32)
    gate_all[me] = jnp.zeros((8, 256), F32)
    ids_in.wait()
    gate_in.wait()
    ids_all[me, :, :tok_dev] = ids_v[...]
    gate_all[me, :, :tok_dev] = gate_v[...]
    pl.semaphore_wait(bar, 7)

    def ids_copy(r):
        return pltpu.make_async_remote_copy(ids_all.at[me], ids_all.at[me], ms_sem, mr_sem,
                                            device_id=dev(r), device_id_type=MESH)

    def gate_copy(r):
        return pltpu.make_async_remote_copy(gate_all.at[me], gate_all.at[me], gs_sem, gr_sem,
                                            device_id=dev(r), device_id_type=MESH)

    def ag_copy(c, kind, mine):
        owner, part, to = AG_KINDS[kind]
        if not mine:
            owner = owner ^ to
        start, size = gidx(owner) * tok_dev, tok_dev
        if part is not None:
            start, size = start + part * half, half
        ref = tok_all.at[c, pl.ds(pl.multiple_of(start, 32), size), :]
        return pltpu.make_async_remote_copy(ref, ref, as_sem, ar_sem.at[c, kind if kind in (1, 2, 3, 4) else 0],
                                            device_id=dev(to), device_id_type=MESH)

    def send_own(c):
        tok_copy(c).wait()
        for kind in (1, 2, 0):
            ag_copy(c, kind, True).start()

    def near(c):
        ag_copy(c, 1, False).wait_recv()
        ag_copy(c, 3, True).start()
        ag_copy(c, 5, True).start()
        ag_copy(c, 2, False).wait_recv()
        ag_copy(c, 4, True).start()
        ag_copy(c, 6, True).start()

    def far(c):
        ag_copy(c, 3, False).wait_recv()
        ag_copy(c, 7, True).start()
        ag_copy(c, 4, False).wait_recv()
        ag_copy(c, 8, True).start()

    for r in range(1, 8):
        ids_copy(r).start()
        gate_copy(r).start()
    for c in range(LEAD):
        send_own(c)
    for p in range(2):
        wi_copy(0, p).start()
    for p in range(2):
        wo_copy(0, p).start()

    def all_of(ref, send, recv):
        return pltpu.make_async_remote_copy(ref, ref, send, recv, device_id=dev(1), device_id_type=MESH)

    all_ids = all_of(ids_all.at[0:7], ms_sem, mr_sem)
    all_gates = all_of(gate_all.at[0:7], gs_sem, gr_sem)
    all_ids.wait_recv()
    all_gates.wait_recv()

    lane = lax.broadcasted_iota(jnp.int32, (8, 128), 1)

    def compact(ref):
        out = []
        for m in range(4):
            a = ref[2 * m]
            b = pltpu.roll(ref[2 * m + 1], 64, 1)
            out += [a[:, :128], jnp.where(lane < 64, a[:, 128:], b[:, :128]), b[:, 128:]]
        return out

    id_blocks, gate_blocks = compact(ids_all), compact(gate_all)
    eid = lax.broadcasted_iota(jnp.int32, (8, 128), 0) + me * nexp
    imasks, gates = [], []
    for idb, gb in zip(id_blocks, gate_blocks):
        m = jnp.zeros((8, 128), jnp.int32)
        g = jnp.zeros((8, 128), F32)
        for k in range(8):
            hit = idb[k:k + 1, :] == eid
            m = jnp.where(hit, 1, m)
            g = jnp.where(hit, gb[k:k + 1, :], g)
        imasks.append(m)
        gates.append(g)
    masks = [m.astype(F32) for m in imasks]
    nb = len(masks)
    tri = jnp.where(lax.broadcasted_iota(jnp.int32, (128, 128), 0) < lax.broadcasted_iota(jnp.int32, (128, 128), 1),
                    1.0, 0.0).astype(BF)
    cums = jnp.dot(jnp.concatenate(masks, axis=0).astype(BF), tri, preferred_element_type=F32)
    carry = jnp.zeros((8, 1), F32)
    ranks = []
    for b in range(nb):
        ranks.append(cums[b * 8:b * 8 + 8, :] + carry)
        carry = carry + jnp.sum(masks[b], axis=1, keepdims=True)
    starts, seen = [], jnp.zeros((8, 128), jnp.int32)
    table = jnp.zeros((8, 128), jnp.int32)
    for g in range(8):
        b = 3 * (g // 2) + g % 2
        before = seen + jnp.where(lane < 64, imasks[b], 0) if g % 2 else seen
        off = jnp.sum(before, axis=1, keepdims=True)
        start16 = jnp.minimum(off >> 4, (cap - WIN) // 16)
        table = jnp.where(lane == g, start16, table)
        starts.append((start16 * 16).astype(F32))
        seen = seen + imasks[b]
        if g % 2:
            seen = seen + imasks[b + 1]
    start_v[...] = table
    st = pltpu.make_async_copy(start_v, start_s, st_sem)
    st.start()
    for b in range(nb):
        m = b // 3
        if b % 3 == 0:
            start = starts[2 * m]
        elif b % 3 == 1:
            start = jnp.where(lane < 64, starts[2 * m], starts[2 * m + 1])
        else:
            start = starts[2 * m + 1]
        keep = (masks[b] > 0.0) & (ranks[b] < float(cap))
        slot_buf[:, b * 128:(b + 1) * 128] = jnp.where(keep, ranks[b], -1.0)
        g1 = gates[b].astype(BF).astype(F32)
        rem1 = gates[b] - g1
        g2 = rem1.astype(BF).astype(F32)
        g3 = rem1 - g2
        zbuf[b, 0:8, :] = jnp.where(keep, ranks[b] - start, -1.0)
        zbuf[b, 8:16, :] = g1
        zbuf[b, 16:24, :] = g2
        zbuf[b, 24:32, :] = g3

    def build_p(e, _):
        row = slot_buf[pl.ds(e, 1), :]
        pos = lax.broadcasted_iota(jnp.int32, (cap, ntok), 0).astype(F32)
        pmat[pl.ds(pl.multiple_of(e * cap, 64), cap), :] = jnp.where(pos == row, 1.0, 0.0).astype(BF)
        return 0

    nwin = nexp * WIN

    def build_c(b, _):
        z = jnp.concatenate([zbuf[b], jnp.zeros((96, 128), F32)], axis=0)
        zt = jnp.transpose(z).astype(BF)
        ex = jnp.where(lax.broadcasted_iota(jnp.int32, (128, 4 * nwin), 0)
                       == lax.broadcasted_iota(jnp.int32, (128, 4 * nwin), 1) // WIN, 1.0, 0.0).astype(BF)
        y = jnp.dot(zt, ex, preferred_element_type=F32)
        wpos = lax.rem(lax.broadcasted_iota(jnp.int32, (128, nwin), 1), WIN).astype(F32)
        hit = y[:, :nwin] == wpos
        rows = pl.ds(pl.multiple_of(b * 128, 128), 128)
        for k in range(3):
            cmat[k, rows, :] = jnp.where(hit, y[:, (k + 1) * nwin:(k + 2) * nwin], 0.0).astype(BF)
        return 0

    def arrived(c):
        all_of(tok_all.at[c, 0:4 * tok_dev, :], as_sem, ar_sem.at[c, 0]).wait_recv()

    def first(c, part):
        experts = range(part * (nexp // 2), (part + 1) * (nexp // 2))
        wi_copy(c, part).wait()

        def dispatch(e):
            return jnp.dot(pmat[e * cap:(e + 1) * cap, :], tok_all[c], preferred_element_type=F32).astype(BF)

        def expand(e, rows):
            y = jnp.dot(rows, wi[part, e % nh], preferred_element_type=F32)
            for n in range(ff // wd):
                yn = y[:, n * wd:(n + 1) * wd]
                if c:
                    yn = yn + hacc[e * (ff // wd) + n]
                if c == nch - 1:
                    hbf[e * cap:(e + 1) * cap, n * wd:(n + 1) * wd] = gelu_tanh(yn).astype(BF)
                else:
                    hacc[e * (ff // wd) + n] = yn

        ready = None
        for e in experts:
            rows = dispatch(e)
            if ready is not None:
                expand(*ready)
            ready = (e, rows)
        expand(*ready)
        if c + 1 < nch:
            wi_copy(c + 1, part).start()

    lax.fori_loop(0, nexp, build_p, 0)
    near(0)
    send_own(2)
    lax.fori_loop(0, nb // 2, build_c, 0)
    near(1)
    send_own(3)
    lax.fori_loop(nb // 2, nb, build_c, 0)
    far(0)
    arrived(0)
    first(0, 0)
    first(0, 1)
    near(2)
    far(1)
    arrived(1)
    first(1, 0)
    near(3)
    first(1, 1)
    far(2)
    arrived(2)
    first(2, 0)
    far(3)
    first(2, 1)
    arrived(3)
    first(3, 0)
    first(3, 1)
    st.wait()

    def d2d_copy(c, q):
        k = c * 4 + q
        return pltpu.make_async_remote_copy(d2d_out.at[k], d2d_in.at[k], ds_sem, dr_sem.at[k],
                                            device_id=dev(1), device_id_type=MESH)

    def hop1(c, axis, k):
        recv = r1_sem.at[c, axis] if k else rf_sem.at[c]
        return pltpu.make_async_remote_copy(out1.at[c, axis, k], in1.at[c, axis, k], s1_sem, recv,
                                            device_id=dev(4 if axis else 2), device_id_type=MESH)

    def hop2(c, part):
        return pltpu.make_async_remote_copy(out2.at[c, part], in2.at[c, part], s2_sem, rf_sem.at[c],
                                            device_id=dev(2 if part else 4), device_id_type=MESH)

    def combine(r):
        g = gidx(r)
        parts = []
        for e in range(nexp):
            at = e * (cap // 16) + start_s[e, g]
            parts.append(obuf[pl.ds(at, WIN // 16)].reshape(WIN, wd))
        win = jnp.concatenate(parts, axis=0)
        rows = pl.ds(pl.multiple_of(g * tok_dev, 64), tok_dev)
        lhs = jnp.concatenate([cmat[k, rows, :] for k in range(3)], axis=0)
        y = jnp.dot(lhs, win, preferred_element_type=F32)
        return y[:tok_dev] + y[tok_dev:2 * tok_dev] + y[2 * tok_dev:]

    def relay(c):
        for part in range(2):
            hop1(c, part, 1).wait_recv()
            out2[c, part] = (kept[c, part] + in1[c, part, 1].astype(F32)).astype(BF)
            hop2(c, part).start()

    def finish(c):
        all_of(in1.at[c], s1_sem, rf_sem.at[c]).wait_recv()
        for part in range(2):
            at = pl.multiple_of(me * tok_dev + part * half, 32)
            y = tok_all[c, pl.ds(at, half), :].astype(F32) + (
                own[c, part] + in1[c, part, 0].astype(F32) + in2[c, part].astype(F32))
            outv[c, part * half:(part + 1) * half, :] = y.astype(BF)
        out_copy(c).start()

    def second(c, _):
        for part in range(2):
            experts = range(part * (nexp // 2), (part + 1) * (nexp // 2))
            wo_copy(c, part).wait()
            for e in experts:
                y = jnp.dot(hbf[e * cap:(e + 1) * cap, :], wo[part, e % nh], preferred_element_type=F32).astype(BF)
                obuf[e * (cap // 16):(e + 1) * (cap // 16)] = y.reshape(cap // 16, 16, wd)

            @pl.when(c + 1 < nch)
            def _():
                wo_copy(c + 1, part).start()

        for pair in ((0, 1), (2, 3)):
            for q in pair:
                d2d_out[c * 4 + q] = combine(RETURN_ORDER[q] + 1).astype(BF)
            for q in pair:
                d2d_copy(c, q).start()
        for q in (0, 1):
            hacc[q] = combine(RETURN_ORDER[q])
        for q, r in enumerate(RETURN_ORDER):
            if q == 2:
                for k in (2, 3):
                    hacc[k] = combine(RETURN_ORDER[k])
            d2d_copy(c, q).wait_recv()
            y = hacc[q] + d2d_in[c * 4 + q].astype(F32)
            if r == 6:
                out1[c, 0, 1] = y[:half].astype(BF)
                out1[c, 1, 1] = y[half:].astype(BF)
                hop1(c, 0, 1).start()
                hop1(c, 1, 1).start()
            elif r == 2:
                out1[c, 0, 0] = y[:half].astype(BF)
                kept[c, 1] = y[half:]
                hop1(c, 0, 0).start()
            elif r == 4:
                out1[c, 1, 0] = y[half:].astype(BF)
                kept[c, 0] = y[:half]
                hop1(c, 1, 0).start()
            else:
                own[c, 0] = y[:half]
                own[c, 1] = y[half:]

        @pl.when(c > 0)
        def _():
            relay(c - 1)

        @pl.when(c > 1)
        def _():
            finish(c - 2)
        return 0

    lax.fori_loop(0, nch, second, 0)
    relay(nch - 1)
    finish(nch - 2)
    finish(nch - 1)

    all_ids.wait_send()
    all_gates.wait_send()
    all_of(tok_all.at[:, 0:7 * tok_dev, :], as_sem, ar_sem.at[0, 0]).wait_send()
    all_of(d2d_out, ds_sem, dr_sem.at[0]).wait_send()
    all_of(out1, s1_sem, rf_sem.at[0]).wait_send()
    all_of(out2, s2_sem, rf_sem.at[0]).wait_send()
    for c in range(nch):
        out_copy(c).wait()


def solution(mesh):
    group_size = mesh.shape['row'] * mesh.shape['col']

    def device_fn(tokens, expert_ids, gate_weights, w_in, w_out):
        tok_dev, width = tokens.shape
        top_k = expert_ids.shape[1]
        nexp, _, ff = w_in.shape
        cap = tok_dev * group_size * top_k // (nexp * group_size)
        ntok = tok_dev * group_size
        nch = 4
        wd = width // nch
        half = tok_dev // 2
        dma = pltpu.SemaphoreType.DMA
        cfg = (tok_dev, cap, nexp, nch, wd, ff)
        hb = pl.BlockSpec(memory_space=pl.ANY)
        return pl.pallas_call(
            functools.partial(moe_kernel, cfg),
            out_shape=jax.ShapeDtypeStruct((tok_dev, width), BF),
            in_specs=[hb] * 5,
            out_specs=hb,
            scratch_shapes=[
                pltpu.VMEM((8, 8, 256), jnp.int32),
                pltpu.VMEM((8, 8, 256), F32),
                pltpu.VMEM((nch, ntok, wd), BF),
                pltpu.VMEM((nexp * cap, ntok), BF),
                pltpu.VMEM((3, ntok, nexp * WIN), BF),
                pltpu.VMEM((nexp * ff // wd, cap, wd), F32),
                pltpu.VMEM((nexp * cap, ff), BF),
                pltpu.VMEM((2, nexp // 2, wd, ff), BF),
                pltpu.VMEM((2, nexp // 2, ff, wd), BF),
                pltpu.VMEM((nexp * cap // 16, 16, wd), BF),
                pltpu.VMEM((nch * 4, tok_dev, wd), BF),
                pltpu.VMEM((nch * 4, tok_dev, wd), BF),
                pltpu.VMEM((nch, 2, 2, half, wd), BF),
                pltpu.VMEM((nch, 2, 2, half, wd), BF),
                pltpu.VMEM((nch, 2, half, wd), BF),
                pltpu.VMEM((nch, 2, half, wd), BF),
                pltpu.VMEM((nch, 2, half, wd), F32),
                pltpu.VMEM((nch, 2, half, wd), F32),
                pltpu.VMEM((nch, tok_dev, wd), BF),
                pltpu.VMEM((8, tok_dev), jnp.int32),
                pltpu.VMEM((8, tok_dev), F32),
                pltpu.VMEM((8, ntok), F32),
                pltpu.VMEM((ntok // 128, 32, 128), F32),
                pltpu.VMEM((8, 128), jnp.int32),
                pltpu.SMEM((8, 128), jnp.int32),
                dma((nch,)), dma((2,)), dma((2,)), dma, dma, dma, dma, dma, dma((nch, 5)), dma, dma((nch * 4,)),
                dma, dma((nch, 2)), dma, dma((nch,)), dma, dma((nch,)), dma, dma,
            ],
            compiler_params=pltpu.CompilerParams(collective_id=0, has_side_effects=True, vmem_limit_bytes=67000000),
        )(expert_ids.T, gate_weights.T, tokens, w_in, w_out)

    token_spec = P(('data', 'row', 'col'), None)
    expert_spec = P(GRID_AXES, None, None)
    return jax.shard_map(device_fn, mesh=mesh, in_specs=(token_spec, token_spec, token_spec, expert_spec, expert_spec),
                         out_specs=token_spec, check_vma=False)
```

profile of v0, /device:TPU:0, one launch (start us, length us, event | category | flops | bytes accessed | tf_op | source)
XLA Modules:
  0.0 78.8 jit_solution(16882849179635021100)
XLA Ops:
  0.0 76.7 %shard_map.55 = bf16[192,2048]{1,0:T(8,128)(2,1)} custom-call(s32[8,192]{1,0:T(8,128)} %bitcast.2, f32[8,192]{1,0:T(8,128)} %bitcast.3, bf16[192,2048]{1,0:T(8,128)(2,1)} %tok_hbm.1, bf16[8,2048,1024]{2,1,0:T(8,128)(2,1)} %wi_hbm.1, bf16[8,1024,2048]{2,1,0:T(8,128)(2,1)} %wo_hbm.1), custom_call_target="tpu_custom_call" | custom-call | tf_op jit(solution)/shard_map/pallas_call | solution.py:414
  76.7 2.1 %copy.7 = bf16[192,2048]{1,0:T(8,128)(2,1)} copy(bf16[192,2048]{1,0:T(8,128)(2,1)} %shard_map.55) | data formatting | bytes 1572864
where the time goes:
time: 79 us; the launch traced here: 78.8 us
  Pallas kernels  76.7 us (97%)
  local copies, waits for them, and re-layouts  2.09 us (3%)
    pallas_call x1, Pallas kernels, device_fn(): pl.pallas_call(functools.partial(moe_kernel, cfg), out_shape=jax.ShapeDty...  76.7 us
    unnamed x1, local copies, waits for them, and re-layouts  2.09 us

commit v1 on v0

--- a/solution.py
+++ b/solution.py
@@ -25,7 +25,7 @@
 
 
 def moe_kernel(cfg, ids_hbm, gate_hbm, tok_hbm, wi_hbm, wo_hbm, out_hbm,
-               ids_all, gate_all, tok_all, pmat, cmat, hacc, hbf, wi, wo, obuf, d2d_out, d2d_in, out1, in1, out2, in2, kept, own, outv,
+               ids_all, gate_all, tok_all, pmat, cmat, hacc, hbf, wi, wo, obuf, d2d_out, d2d_in, out1, in1, out2, in2, kept, own,
                ids_v, gate_v, slot_buf, zbuf, start_v, start_s,
                tok_sem, wi_sem, wo_sem, ms_sem, mr_sem, gs_sem, gr_sem, as_sem, ar_sem, ds_sem, dr_sem,
                s1_sem, r1_sem, s2_sem, rf_sem, st_sem, out_sem, id_sem, gate_sem):
@@ -69,7 +69,7 @@
                                      wo_sem.at[p])
 
     def out_copy(c):
-        return pltpu.make_async_copy(outv.at[c], out_hbm.at[:, pl.ds(pl.multiple_of(c * wd, wd), wd)], out_sem.at[c])
+        return pltpu.make_async_copy(own.at[c], out_hbm.at[:, :, pl.ds(pl.multiple_of(c * wd, wd), wd)], out_sem.at[c])
 
     bar = pltpu.get_barrier_semaphore()
     for r in range(1, 8):
@@ -324,10 +324,7 @@
     def finish(c):
         all_of(in1.at[c], s1_sem, rf_sem.at[c]).wait_recv()
         for part in range(2):
-            at = pl.multiple_of(me * tok_dev + part * half, 32)
-            y = tok_all[c, pl.ds(at, half), :].astype(F32) + (
-                own[c, part] + in1[c, part, 0].astype(F32) + in2[c, part].astype(F32))
-            outv[c, part * half:(part + 1) * half, :] = y.astype(BF)
+            own[c, part] = own[c, part] + in1[c, part, 0].astype(F32) + in2[c, part].astype(F32)
         out_copy(c).start()
 
     def second(c, _):
@@ -411,9 +408,9 @@
         dma = pltpu.SemaphoreType.DMA
         cfg = (tok_dev, cap, nexp, nch, wd, ff)
         hb = pl.BlockSpec(memory_space=pl.ANY)
-        return pl.pallas_call(
+        mixed = pl.pallas_call(
             functools.partial(moe_kernel, cfg),
-            out_shape=jax.ShapeDtypeStruct((tok_dev, width), BF),
+            out_shape=jax.ShapeDtypeStruct((2, half, width), F32),
             in_specs=[hb] * 5,
             out_specs=hb,
             scratch_shapes=[
@@ -435,7 +432,6 @@
                 pltpu.VMEM((nch, 2, half, wd), BF),
                 pltpu.VMEM((nch, 2, half, wd), F32),
                 pltpu.VMEM((nch, 2, half, wd), F32),
-                pltpu.VMEM((nch, tok_dev, wd), BF),
                 pltpu.VMEM((8, tok_dev), jnp.int32),
                 pltpu.VMEM((8, tok_dev), F32),
                 pltpu.VMEM((8, ntok), F32),
@@ -447,6 +443,7 @@
             ],
             compiler_params=pltpu.CompilerParams(collective_id=0, has_side_effects=True, vmem_limit_bytes=67000000),
         )(expert_ids.T, gate_weights.T, tokens, w_in, w_out)
+        return (tokens.astype(F32) + mixed.reshape(tok_dev, width)).astype(BF)
 
     token_spec = P(('data', 'row', 'col'), None)
     expert_spec = P(GRID_AXES, None, None)

time: 79 us -> 79.6 us (level)
  other arithmetic: 0 us -> 2.67 us
  local copies, waits for them, and re-layouts: 2.09 us -> 0 us
    convert_element_type x0 -> x1, other arithmetic: none -> 2.67 us  [device_fn(): return (tokens.astype(F32) + mixed.reshape(tok_dev, width)).astype(BF)]
    unnamed x1 -> x0, local copies, waits for them, and re-layouts: 2.09 us -> none
where the time goes in v1:
time: 79.6 us; the launch traced here: 79.5 us
  Pallas kernels  76.8 us (96%)
  other arithmetic  2.67 us (3%)
    pallas_call x1, Pallas kernels, device_fn(): pl.pallas_call(functools.partial(moe_kernel, cfg), out_shape=jax.ShapeDty...  76.8 us
    convert_element_type x1, other arithmetic, device_fn(): return (tokens.astype(F32) + mixed.reshape(tok_dev, width)).astype(BF)  2.67 us

profile of v1, /device:TPU:0, one launch (start us, length us, event | category | flops | bytes accessed | tf_op | source)
XLA Modules:
  0.0 79.5 jit_solution(3408910261279529784)
XLA Ops:
  0.0 76.8 %shard_map.55 = f32[2,96,2048]{2,1,0:T(8,128)} custom-call(s32[8,192]{1,0:T(8,128)} %bitcast.6, f32[8,192]{1,0:T(8,128)} %bitcast.7, bf16[192,2048]{1,0:T(8,128)(2,1)} %tok_hbm.1, bf16[8,2048,1024]{2,1,0:T(8,128)(2,1)} %wi_hbm.1, bf16[8,1024,2048]{2,1,0:T(8,128)(2,1)} %wo_hbm.1), custom_call_target="tpu_custom_call" | custom-call | tf_op jit(solution)/shard_map/pallas_call | solution.py:411
  76.8 2.7 %fusion = bf16[192,2048]{1,0:T(8,128)(2,1)} fusion(f32[2,96,2048]{2,1,0:T(8,128)} %shard_map.55, bf16[192,2048]{1,0:T(8,128)(2,1)} %tok_hbm.1), kind=kLoop, calls=%fused_computation.1 | loop fusion | flops 1179648 | bytes 3145728 | tf_op jit(solution)/shard_map/convert_element_type | solution.py:446
